TPU v7x, 32 devices: a whole 2x2x4 slice. The times are simulated.
32 devices in a mesh: src: 4 (over y, x), blk: 8 (over z, core).
Axes of the slice: x: 2, y: 2, z: 4, core: 2. Of those that a mesh axis runs over, the one named last changes fastest.
Arguments:
- values: float32 [4, 512, 32, 128], P('src', 'blk'), may hold values from -0.25 to 0.25
- diagonal: float32 [4, 512, 128], P('src', 'blk'), may hold values from 0.55 to 0.95
- rhs_parts: float32 [4, 512, 128], P('src', 'blk'), may hold values from -24 to 24
- owner_map: int32 [512, 128], P('blk'), may hold values from 0 to 3
- columns: int32 [512, 32, 128], P('blk'), may hold values from 0 to 1073741823
- destination: int32 [512, 1], P('blk'), may hold values from 0 to 7; in each aligned block of 64 rows (0 to 63, 64 to 127, ...) at most 16 rows name the same one
- order_keys: int32 [512], P('blk'), may hold values from 0 to 511, each once
Outputs:
- solution: float32 [512, 128], P('blk')
Inputs may be any that keep to these rules, and one draw needn't show every extreme that they name: `destination`: among the row blocks of one index of blk no owner is named more than 16 times, some owner is named exactly 16 times, and every owner is named by some block. `order_keys`: each key appears once.
All inputs are finite; a program needn't handle non-finite values.
Results may differ from a plain program's by a relative error of at most 0.0003.
Values sent between devices are 32-bit elements; how exact they have to be, the bound alone decides.
No kernel may reach another device: no remote copies, remote signals or barrier semaphores. Data moves between devices by JAX's collectives and lax.ppermute only.
A program may use at most 64 MiB of HBM per device.

v0:
```python
import jax
import jax.numpy as jnp
from jax import lax
from jax.sharding import PartitionSpec as P

SWEEPS = 3


def tile_matrix(block_vals, block_cols, tile_rows):
    slot_count = block_vals.shape[0]
    stored = block_vals.shape[1]
    groups = 8
    lanes = jnp.remainder(block_cols, 2 * tile_rows)
    targets = jnp.arange(2 * tile_rows, dtype=jnp.int32)
    grouped_vals = block_vals.reshape(groups, slot_count // groups, stored, tile_rows)
    grouped_lanes = lanes.reshape(groups, slot_count // groups, stored, tile_rows)

    def build(pair):
        group_vals, group_lanes = pair
        picked = jnp.where(group_lanes[..., None] == targets, group_vals[..., None], 0.0)
        return jnp.sum(picked, axis=1)

    dense = lax.map(build, (grouped_vals, grouped_lanes))
    return dense.reshape(slot_count, tile_rows, 2 * tile_rows)


def on_device(values, diagonal, rhs_parts, owner_map, columns, destination, order_keys):
    owners = lax.axis_size("blk")
    part_count = lax.axis_size("src")
    tile_count = destination.shape[0]
    stored = values.shape[2]
    tile_rows = values.shape[3]
    per_peer = 2 * tile_count // owners
    slot_count = owners * per_peer
    owner_of = destination[:, 0]
    tile_ids = jnp.arange(tile_count, dtype=jnp.int32)
    slot_ids = jnp.arange(slot_count, dtype=jnp.int32)
    earlier = (owner_of[None, :] == owner_of[:, None]) & (tile_ids[None, :] < tile_ids[:, None])
    position = jnp.sum(earlier, axis=1)
    slot_of = owner_of * per_peer + position
    slot_hits = slot_of[None, :] == slot_ids[:, None]
    filled = jnp.any(slot_hits, axis=1)
    source_tile = jnp.sum(jnp.where(slot_hits, tile_ids[None, :], 0), axis=1)
    is_owned = owner_map == lax.axis_index("src")
    own_rhs = jnp.where(is_owned, rhs_parts[0], 0.0)
    send_vals = jnp.where(filled[:, None, None], values[0][source_tile], 0.0)
    send_diag = jnp.where(filled[:, None], diagonal[0][source_tile], 0.0)
    send_rhs = jnp.where(filled[:, None], own_rhs[source_tile], 0.0)
    send_cols = columns[source_tile]
    send_keys = jnp.where(filled, order_keys[source_tile], -1)
    quarter = stored // part_count
    part_vals = lax.psum_scatter(send_vals, "src", scatter_dimension=1, tiled=True)
    sum_diag, sum_rhs = lax.psum((send_diag, send_rhs), "src")
    part_cols = lax.dynamic_slice_in_dim(send_cols, lax.axis_index("src") * quarter, quarter, 1)
    got_vals, got_diag, got_rhs = (
        lax.all_to_all(part_vals, "blk", split_axis=0, concat_axis=0, tiled=True),
        lax.all_to_all(sum_diag, "blk", split_axis=0, concat_axis=0, tiled=True),
        lax.all_to_all(sum_rhs, "blk", split_axis=0, concat_axis=0, tiled=True),
    )
    got_cols, got_keys = (
        lax.all_to_all(part_cols, "blk", split_axis=0, concat_axis=0, tiled=True),
        lax.all_to_all(send_keys, "blk", split_axis=0, concat_axis=0, tiled=True),
    )
    is_live = got_keys >= 0
    tile_total = jnp.sum(is_live)
    smaller = is_live[None, :] & (got_keys[None, :] < got_keys[:, None])
    tile_rank = jnp.sum(smaller, axis=1)
    rank_hits = is_live[None, :] & (tile_rank[None, :] == slot_ids[:, None])
    holder = jnp.sum(jnp.where(rank_hits, slot_ids[None, :], 0), axis=1)
    occupied = slot_ids < tile_total
    block_vals = jnp.where(occupied[:, None, None], got_vals[holder], 0.0)
    block_cols = got_cols[holder]
    right_side = jnp.where(occupied[:, None], got_rhs[holder], 0.0)
    block_diag = jnp.where(occupied[:, None], got_diag[holder], 1.0)
    dense = tile_matrix(block_vals, block_cols, tile_rows)
    following = jnp.remainder(slot_ids + 1, tile_total)
    iterate = jnp.zeros((slot_count, tile_rows), jnp.float32)
    for sweep_index in range(SWEEPS):
        nearby = jnp.concatenate([iterate, iterate[following]], axis=1)
        partial_sum = jnp.sum(dense * nearby[:, None, :], axis=2)
        summed = lax.psum(partial_sum, "src")
        iterate = jnp.where(occupied[:, None], (right_side - summed) / block_diag, 0.0)
    in_slots = jnp.where(is_live[:, None], iterate[tile_rank], 0.0)
    returned = lax.all_to_all(in_slots, "blk", split_axis=0, concat_axis=0, tiled=True)
    return returned[slot_of]


def solution(mesh):
    placed = (
        P("src", "blk", None, None),
        P("src", "blk", None),
        P("src", "blk", None),
        P("blk", None),
        P("blk", None, None),
        P("blk", None),
        P("blk"),
    )
    return jax.shard_map(
        on_device, mesh=mesh, in_specs=placed, out_specs=P("blk", None), check_vma=False
    )
```

profile of v0, /device:TPU:0, one launch (start us, length us, event | category | flops | bytes accessed | tf_op | source)
XLA Modules:
  0.0 320.4 jit_solution(3956767261336183481)
XLA Ops:
  6.6 0.9 convert_reduce_fusion.1
  7.5 0.7 multiply_add_fusion
  8.4 0.8 gather_fusion.5
  9.2 1.6 broadcast_select_fusion
  10.8 1.6 gather_fusion
  12.4 0.7 select_n.147
  13.1 6.4 %all-to-all-start = ((s32[8,16,1]{1,2,0:T(1,128)}), s32[8,16,1]{1,2,0:T(1,128)S(1)}, u32[]{:S(2)}, u32[]{:S(2)}) async-start(s32[8,16,1]{1,2,0:T(1,128)} %bitcast.3), calls=%async_computation | async-start | bytes 8192 | tf_op jit(solution)/shard_map/all_to_all | solution.py:62
  19.4 2.2 gather_fusion.3
  21.6 0.9 constant_dynamic-slice_fusion
  22.5 2.4 all-to-all-done
  24.9 3.5 %all-to-all-start.2 = ((s32[128,8,128]{2,1,0:T(8,128)}), s32[128,8,128]{2,1,0:T(8,128)S(1)}, u32[]{:S(2)}, u32[]{:S(2)}) async-start(s32[128,8,128]{2,1,0:T(8,128)} %constant_dynamic-slice_fusion), calls=%async_computation.2 | async-start | bytes 1048576 | tf_op jit(solution)/shard_map/all_to_all | solution.py:61
  28.5 0.6 gather_fusion.1
  29.1 0.6 gather_fusion.8
  29.8 0.7 broadcast_select_fusion.4
  30.5 0.5 broadcast.232
  31.0 0.7 reduce.7
  31.8 0.6 convert_reduce_fusion.2
  33.9 0.6 gather_fusion.7
  34.5 9.2 %all-to-all-done.2 = s32[128,8,128]{2,1,0:T(8,128)S(1)} async-done(((s32[128,8,128]{2,1,0:T(8,128)}), s32[128,8,128]{2,1,0:T(8,128)S(1)}, u32[]{:S(2)}, u32[]{:S(2)}) %all-to-all-start.2) | async-done | bytes 524320 | tf_op jit(solution)/shard_map/all_to_all | solution.py:61
  43.7 5.2 %reduce-scatter.2.cloned.1.call-done = f32[128,8,128]{2,1,0:T(8,128)} async-done(((f32[128,32,128]{2,1,0:T(8,128)}), f32[128,8,128]{2,1,0:T(8,128)}) %reduce-scatter.2.cloned.1.call-update) | async-done | bytes 524304 | tf_op jit(solution)/shard_map/reduce_scatter | solution.py:52
  48.9 4.6 %all-to-all-start.3 = ((f32[128,8,128]{2,1,0:T(8,128)}), f32[128,8,128]{2,1,0:T(8,128)S(1)}, u32[]{:S(2)}, u32[]{:S(2)}) async-start(f32[128,8,128]{2,1,0:T(8,128)} %reduce-scatter.2.cloned.1.call-done), calls=%async_computation.4 | async-start | bytes 1048576 | tf_op jit(solution)/shard_map/all_to_all | solution.py:56
  53.5 0.7 add_compare_fusion
  54.5 0.8 gather_fusion.4
  55.5 13.3 %all-to-all-done.3 = f32[128,8,128]{2,1,0:T(8,128)S(1)} async-done(((f32[128,8,128]{2,1,0:T(8,128)}), f32[128,8,128]{2,1,0:T(8,128)S(1)}, u32[]{:S(2)}, u32[]{:S(2)}) %all-to-all-start.3) | async-done | bytes 524320 | tf_op jit(solution)/shard_map/all_to_all | solution.py:56
  68.8 0.8 gather_fusion.6
  69.8 57.8 %while.11 = (s32[]{:T(128)}, f32[8,16,128,256]{3,2,1,0:T(8,128)}, s32[8,16,8,128]{3,2,1,0:T(8,128)S(1)}, f32[8,16,8,128]{3,2,1,0:T(8,128)S(1)}, s32[]{:T(128)}) while((s32[]{:T(128)}, f32[8,16,128,256]{3,2,1,0:T(8,128)}, s32[8,16,8,128]{3,2,1,0:T(8,128)S(1)}, f32[8,16,8,128]{3,2,1,0:T(8,128)S(1)}, s32[]{:T(128)}) %tuple.23), condition=%wide.region_10.11_spmd.clone, body=%wide.region_8.10_spmd.clone.sunk | while | flops 12058626 | bytes 6685253 | solution.py:23
  69.8 5.7 %select_reduce_fusion.4 = f32[16,128,256]{2,1,0:T(8,128)S(1)} fusion(f32[16,8,128]{2,1,0:T(8,128)S(1)} %dynamic-slice_bitcast_fusion.4, s32[16,8,128]{2,1,0:T(8,128)S(1)} %dynamic-slice_bitcast_fusion.5), kind=kLoop, calls=%fused_computation.16.clone.1 | loop fusion | flops 12058624 | bytes 2228224 | tf_op jit(solution)/shard_map/while/body/eval_jaxpr/reduce_sum | solution.py:21
  75.5 1.6 bitcast_dynamic-update-slice_fusion.2
  77.1 5.7 %select_reduce_fusion.4 = f32[16,128,256]{2,1,0:T(8,128)S(1)} fusion(f32[16,8,128]{2,1,0:T(8,128)S(1)} %dynamic-slice_bitcast_fusion.4, s32[16,8,128]{2,1,0:T(8,128)S(1)} %dynamic-slice_bitcast_fusion.5), kind=kLoop, calls=%fused_computation.16.clone.1 | loop fusion | flops 12058624 | bytes 2228224 | tf_op jit(solution)/shard_map/while/body/eval_jaxpr/reduce_sum | solution.py:21
  82.7 1.5 bitcast_dynamic-update-slice_fusion.2
  84.2 5.7 %select_reduce_fusion.4 = f32[16,128,256]{2,1,0:T(8,128)S(1)} fusion(f32[16,8,128]{2,1,0:T(8,128)S(1)} %dynamic-slice_bitcast_fusion.4, s32[16,8,128]{2,1,0:T(8,128)S(1)} %dynamic-slice_bitcast_fusion.5), kind=kLoop, calls=%fused_computation.16.clone.1 | loop fusion | flops 12058624 | bytes 2228224 | tf_op jit(solution)/shard_map/while/body/eval_jaxpr/reduce_sum | solution.py:21
  89.9 1.5 bitcast_dynamic-update-slice_fusion.2
  91.5 5.7 %select_reduce_fusion.4 = f32[16,128,256]{2,1,0:T(8,128)S(1)} fusion(f32[16,8,128]{2,1,0:T(8,128)S(1)} %dynamic-slice_bitcast_fusion.4, s32[16,8,128]{2,1,0:T(8,128)S(1)} %dynamic-slice_bitcast_fusion.5), kind=kLoop, calls=%fused_computation.16.clone.1 | loop fusion | flops 12058624 | bytes 2228224 | tf_op jit(solution)/shard_map/while/body/eval_jaxpr/reduce_sum | solution.py:21
  97.1 1.5 bitcast_dynamic-update-slice_fusion.2
  98.7 5.7 %select_reduce_fusion.4 = f32[16,128,256]{2,1,0:T(8,128)S(1)} fusion(f32[16,8,128]{2,1,0:T(8,128)S(1)} %dynamic-slice_bitcast_fusion.4, s32[16,8,128]{2,1,0:T(8,128)S(1)} %dynamic-slice_bitcast_fusion.5), kind=kLoop, calls=%fused_computation.16.clone.1 | loop fusion | flops 12058624 | bytes 2228224 | tf_op jit(solution)/shard_map/while/body/eval_jaxpr/reduce_sum | solution.py:21
  104.4 1.6 bitcast_dynamic-update-slice_fusion.2
  106.0 5.7 %select_reduce_fusion.4 = f32[16,128,256]{2,1,0:T(8,128)S(1)} fusion(f32[16,8,128]{2,1,0:T(8,128)S(1)} %dynamic-slice_bitcast_fusion.4, s32[16,8,128]{2,1,0:T(8,128)S(1)} %dynamic-slice_bitcast_fusion.5), kind=kLoop, calls=%fused_computation.16.clone.1 | loop fusion | flops 12058624 | bytes 2228224 | tf_op jit(solution)/shard_map/while/body/eval_jaxpr/reduce_sum | solution.py:21
  111.6 1.5 bitcast_dynamic-update-slice_fusion.2
  113.1 5.7 %select_reduce_fusion.4 = f32[16,128,256]{2,1,0:T(8,128)S(1)} fusion(f32[16,8,128]{2,1,0:T(8,128)S(1)} %dynamic-slice_bitcast_fusion.4, s32[16,8,128]{2,1,0:T(8,128)S(1)} %dynamic-slice_bitcast_fusion.5), kind=kLoop, calls=%fused_computation.16.clone.1 | loop fusion | flops 12058624 | bytes 2228224 | tf_op jit(solution)/shard_map/while/body/eval_jaxpr/reduce_sum | solution.py:21
  118.8 1.6 bitcast_dynamic-update-slice_fusion.2
  120.4 5.7 %select_reduce_fusion.4 = f32[16,128,256]{2,1,0:T(8,128)S(1)} fusion(f32[16,8,128]{2,1,0:T(8,128)S(1)} %dynamic-slice_bitcast_fusion.4, s32[16,8,128]{2,1,0:T(8,128)S(1)} %dynamic-slice_bitcast_fusion.5), kind=kLoop, calls=%fused_computation.16.clone.1 | loop fusion | flops 12058624 | bytes 2228224 | tf_op jit(solution)/shard_map/while/body/eval_jaxpr/reduce_sum | solution.py:21
  126.1 1.5 bitcast_dynamic-update-slice_fusion.2
  127.6 8.6 %multiply_reduce_fusion.2 = f32[8,16,128]{2,1,0:T(8,128)} fusion(f32[8,16,128,256]{3,2,1,0:T(8,128)} %get-tuple-element.32, f32[8,16,256]{2,1,0:T(8,128)S(1)} %bitcast.63), kind=kLoop, calls=%fused_computation.22 | loop fusion | flops 8372224 | bytes 16973824 | tf_op jit(solution)/shard_map/reduce_sum | solution.py:80
  136.2 41.3 %all-reduce.10.cloned.1.call-done = (f32[128,128]{1,0:T(8,128)}, f32[8,16,128]{2,1,0:T(8,128)}, f32[8,16,128]{2,1,0:T(8,128)}) async-done(((f32[128,128]{1,0:T(8,128)}, f32[8,16,128]{2,1,0:T(8,128)}, f32[8,16,128]{2,1,0:T(8,128)}), (f32[128,128]{1,0:T(8,128)}, f32[8,16,128]{2,1,0:T(8,128)}, f32[8,16,128]{2,1,0:T(8,128)})) %all-reduce.10.cloned.1.call-update) | async-done | bytes 196624 | tf_op jit(solution)/shard_map/psum | solution.py:81
  177.5 10.5 %all_to_all.52 = f32[8,16,128]{2,1,0:T(8,128)S(1)} all-to-all(f32[8,16,128]{2,1,0:T(8,128)} %get-tuple-element.53), channel_id=1, replica_groups=mesh['src'=4,'blk'=8] {'blk'}, dimensions={0} | all-to-all | bytes 131072 | tf_op jit(solution)/shard_map/all_to_all | solution.py:58
  188.0 3.3 %all-to-all-start.4 = ((f32[8,16,128]{2,1,0:T(8,128)}), f32[8,16,128]{2,1,0:T(8,128)S(1)}, u32[]{:S(2)}, u32[]{:S(2)}) async-start(f32[8,16,128]{2,1,0:T(8,128)} %get-tuple-element.52), calls=%async_computation.5 | async-start | bytes 131072 | tf_op jit(solution)/shard_map/all_to_all | solution.py:57
  191.4 0.7 iota_compare_fusion.4
  192.1 0.6 gather_fusion.2
  192.7 4.5 %all-to-all-done.4 = f32[8,16,128]{2,1,0:T(8,128)S(1)} async-done(((f32[8,16,128]{2,1,0:T(8,128)}), f32[8,16,128]{2,1,0:T(8,128)S(1)}, u32[]{:S(2)}, u32[]{:S(2)}) %all-to-all-start.4) | async-done | bytes 65568 | tf_op jit(solution)/shard_map/all_to_all | solution.py:57
  197.2 0.6 gather_fusion.9
  197.9 0.9 divide_select_fusion.2
  198.8 0.6 gather_fusion.10
  199.5 8.6 %multiply_reduce_fusion.1 = f32[8,16,128]{2,1,0:T(8,128)} fusion(f32[8,16,128,256]{3,2,1,0:T(8,128)} %get-tuple-element.32, f32[8,16,256]{2,1,0:T(8,128)S(1)} %bitcast.65), kind=kLoop, calls=%fused_computation.21 | loop fusion | flops 8372224 | bytes 16973824 | tf_op jit(solution)/shard_map/reduce_sum | solution.py:80
  208.4 39.3 %all-reduce.6.cloned.1.call-done = f32[128,128]{1,0:T(8,128)} async-done(((f32[128,128]{1,0:T(8,128)}), f32[128,128]{1,0:T(8,128)}) %all-reduce.6.cloned.1.call-update) | async-done | bytes 65552 | tf_op jit(solution)/shard_map/psum | solution.py:81
  247.7 0.9 divide_select_fusion.1
  248.6 0.6 gather_fusion.11
  249.2 8.6 %multiply_reduce_fusion = f32[8,16,128]{2,1,0:T(8,128)} fusion(f32[8,16,128,256]{3,2,1,0:T(8,128)} %get-tuple-element.32, f32[8,16,256]{2,1,0:T(8,128)S(1)} %bitcast.64), kind=kLoop, calls=%fused_computation.20 | loop fusion | flops 8372224 | bytes 16973824 | tf_op jit(solution)/shard_map/reduce_sum | solution.py:80
  257.9 42.0 %all-reduce.8.cloned.1.call-done = f32[128,128]{1,0:T(8,128)} async-done(((f32[128,128]{1,0:T(8,128)}), f32[128,128]{1,0:T(8,128)}) %all-reduce.8.cloned.1.call-update) | async-done | bytes 65552 | tf_op jit(solution)/shard_map/psum | solution.py:81
  299.9 0.9 divide_select_fusion
  300.8 0.6 gather_fusion.12
  301.5 0.7 broadcast_select_fusion.2
  302.2 4.6 %all-to-all-start.5 = ((f32[8,16,128]{2,1,0:T(8,128)}), f32[8,16,128]{2,1,0:T(8,128)S(1)}, u32[]{:S(2)}, u32[]{:S(2)}) async-start(f32[8,16,128]{2,1,0:T(8,128)} %broadcast_select_fusion.2), calls=%async_computation.6 | async-start | bytes 131072 | tf_op jit(solution)/shard_map/all_to_all | solution.py:84
  306.8 5.9 %all-to-all-done.5 = f32[8,16,128]{2,1,0:T(8,128)S(1)} async-done(((f32[8,16,128]{2,1,0:T(8,128)}), f32[8,16,128]{2,1,0:T(8,128)S(1)}, u32[]{:S(2)}, u32[]{:S(2)}) %all-to-all-start.5) | async-done | bytes 65568 | tf_op jit(solution)/shard_map/all_to_all | solution.py:84
  312.7 1.2 gather_fusion.13
  (59 shorter events, 1.7 us)
Async XLA Ops:
  6.5 1.9 copy-start
  6.5 21.9 %copy-start.2 = (f32[1,64,128]{2,1,0:T(8,128)S(1)}, f32[1,64,128]{2,1,0:T(8,128)}, u32[]{:S(2)}) copy-start(f32[1,64,128]{2,1,0:T(8,128)} %param.11) | copy-start | bytes 98308
  6.5 21.9 %copy-start.3 = (s32[64,128]{1,0:T(8,128)S(1)}, s32[64,128]{1,0:T(8,128)}, u32[]{:S(2)}) copy-start(s32[64,128]{1,0:T(8,128)} %param.12) | copy-start | bytes 98308
  6.5 22.6 %copy-start.1 = (f32[1,64,128]{2,1,0:T(8,128)S(1)}, f32[1,64,128]{2,1,0:T(8,128)}, u32[]{:S(2)}) copy-start(f32[1,64,128]{2,1,0:T(8,128)} %param.10) | copy-start | bytes 98308
  6.5 42.3 %reduce-scatter.2.cloned.1.call-start = ((), (), s32[]{:S(2)}) async-start(), calls=%async_computation.7 | async-start | bytes 2621440 | tf_op jit(solution)/shard_map/reduce_scatter | solution.py:52
  13.1 11.9 %all-to-all-start = ((s32[8,16,1]{1,2,0:T(1,128)}), s32[8,16,1]{1,2,0:T(1,128)S(1)}, u32[]{:S(2)}, u32[]{:S(2)}) async-start(s32[8,16,1]{1,2,0:T(1,128)} %bitcast.3), calls=%async_computation | async-start | bytes 8192 | tf_op jit(solution)/shard_map/all_to_all | solution.py:62
  24.9 18.8 %all-to-all-start.2 = ((s32[128,8,128]{2,1,0:T(8,128)}), s32[128,8,128]{2,1,0:T(8,128)S(1)}, u32[]{:S(2)}, u32[]{:S(2)}) async-start(s32[128,8,128]{2,1,0:T(8,128)} %constant_dynamic-slice_fusion), calls=%async_computation.2 | async-start | bytes 1048576 | tf_op jit(solution)/shard_map/all_to_all | solution.py:61
  48.9 19.9 %all-to-all-start.3 = ((f32[128,8,128]{2,1,0:T(8,128)}), f32[128,8,128]{2,1,0:T(8,128)S(1)}, u32[]{:S(2)}, u32[]{:S(2)}) async-start(f32[128,8,128]{2,1,0:T(8,128)} %reduce-scatter.2.cloned.1.call-done), calls=%async_computation.4 | async-start | bytes 1048576 | tf_op jit(solution)/shard_map/all_to_all | solution.py:56
  53.5 124.0 %all-reduce.10.cloned.1.call-start = ((), (), s32[]{:S(2)}) async-start(), calls=%async_computation.10 | async-start | bytes 393216 | tf_op jit(solution)/shard_map/psum | solution.py:81
  188.0 9.2 %all-to-all-start.4 = ((f32[8,16,128]{2,1,0:T(8,128)}), f32[8,16,128]{2,1,0:T(8,128)S(1)}, u32[]{:S(2)}, u32[]{:S(2)}) async-start(f32[8,16,128]{2,1,0:T(8,128)} %get-tuple-element.52), calls=%async_computation.5 | async-start | bytes 131072 | tf_op jit(solution)/shard_map/all_to_all | solution.py:57
  191.4 56.3 %all-reduce.6.cloned.1.call-start = ((), (), s32[]{:S(2)}) async-start(), calls=%async_computation.8 | async-start | bytes 131072 | tf_op jit(solution)/shard_map/psum | solution.py:81
  199.5 107.3 %copy-start.4 = (s32[64,1]{0,1:T(1,128)S(1)}, s32[64,1]{0,1:T(1,128)}, u32[]{:S(2)}) copy-start(s32[64,1]{0,1:T(1,128)} %param.14) | copy-start | bytes 772
  208.1 91.8 %all-reduce.8.cloned.1.call-start = ((), (), s32[]{:S(2)}) async-start(), calls=%async_computation.9 | async-start | bytes 131072 | tf_op jit(solution)/shard_map/psum | solution.py:81
  302.2 10.5 %all-to-all-start.5 = ((f32[8,16,128]{2,1,0:T(8,128)}), f32[8,16,128]{2,1,0:T(8,128)S(1)}, u32[]{:S(2)}, u32[]{:S(2)}) async-start(f32[8,16,128]{2,1,0:T(8,128)} %broadcast_select_fusion.2), calls=%async_computation.6 | async-start | bytes 131072 | tf_op jit(solution)/shard_map/all_to_all | solution.py:84
Sparse Core Ops, SparseCore 0:
  10.9 37.9 reduce-scatter.1
  136.4 41.0 all-reduce.9
  208.2 39.3 all-reduce.5
  258.0 41.8 all-reduce.7
where the time goes:
time: 321 us; the launch traced here: 320 us
  waiting for transfers between devices  163 us (51%)
  other arithmetic  82.2 us (26%)
  local copies, waits for them, and re-layouts  27 us (8%)
  starting transfers between devices  22.7 us (7%)
  between operations  14.7 us (5%)
  blocking collectives  10.5 us (3%)
    psum x3, waiting for transfers between devices, on_device(): summed = lax.psum(partial_sum, 'src')  123 us
    reduce_sum x8, other arithmetic, build(): return jnp.sum(picked, axis=1)  45.3 us
    reduce_sum x3, other arithmetic, on_device(): partial_sum = jnp.sum(dense * nearby[:, None, :], axis=2)  25.9 us
    all_to_all x1, waiting for transfers between devices, on_device(): lax.all_to_all(part_vals, 'blk', split_axis=0, concat_axis=0, tiled=True)  13.3 us
    dynamic_update_slice x8, local copies, waits for them, and re-layouts, tile_matrix(): dense = lax.map(build, (grouped_vals, grouped_lanes))  12.3 us
    all_to_all x1, blocking collectives, on_device(): lax.all_to_all(sum_rhs, 'blk', split_axis=0, concat_axis=0, tiled=True)  10.5 us
    all_to_all x1, waiting for transfers between devices, on_device(): lax.all_to_all(part_cols, 'blk', split_axis=0, concat_axis=0, tiled=True)  9.16 us
  transfers between devices with their start and end apart: 9, of which 9 were waited for; matrix products, arithmetic and copies ran while one was open for 4% of the time, Pallas kernels for 0%

commit v1 on v0

v1 whole, which is shorter than its diff:
```python
import jax
import jax.numpy as jnp
from jax import lax
from jax.experimental import pallas as pl
from jax.experimental.pallas import tpu as pltpu
from jax.sharding import PartitionSpec as P

SWEEPS = 3
BOTH = ("src", "blk")
HEAD = 8


def start_kernel(small_ref, owner_ref, head_ref, diag_out, right_out, send_out):
    parts = small_ref.shape[0]
    rows = diag_out.shape[0]
    owner = owner_ref[...]
    diag = small_ref[0, 0]
    right = jnp.where(owner == 0, small_ref[0, 1], 0.0)
    for part in range(1, parts):
        diag = diag + small_ref[part, 0]
        right = jnp.where(owner == part, small_ref[part, 1], right)
    diag_out[...] = diag
    right_out[...] = right
    first = right / diag
    send_out[:, :rows] = jnp.broadcast_to(first[None], (send_out.shape[0],) + first.shape)
    send_out[:, rows:] = jnp.broadcast_to(head_ref[...][None], (send_out.shape[0], HEAD, first.shape[1]))


def gather_tile(own, following, codes, rows):
    lanes = codes & (rows - 1)
    here = jnp.take_along_axis(jnp.broadcast_to(own, codes.shape), lanes, axis=1)
    there = jnp.take_along_axis(jnp.broadcast_to(following, codes.shape), lanes, axis=1)
    return jnp.where((codes & rows) == 0, here, there)


def follow(pick, everyone):
    return jnp.dot(pick, everyone, precision=lax.Precision.HIGHEST, preferred_element_type=jnp.float32)


def nearby_kernel(got_ref, own_ref, owner_ref, key_ref, codes_ref, nearby_out, pick_out, least_ref):
    tiles, _, rows = codes_ref.shape
    peers = got_ref.shape[0]
    total = peers * tiles
    owners = got_ref[:, tiles, :]
    keys = got_ref[:, tiles + 1, :]
    place = lax.broadcasted_iota(jnp.int32, owners.shape, 0) * tiles + lax.broadcasted_iota(jnp.int32, owners.shape, 1)
    place = place.astype(jnp.float32)
    for tile in range(tiles):
        ahead = keys - key_ref[tile:tile + 1, 0:1] - 1.0
        ahead = jnp.where(ahead < 0.0, ahead + total, ahead)
        code = jnp.where(owners == owner_ref[tile:tile + 1, 0:1], ahead * total + place, float(total * total))
        least_ref[tile:tile + 1] = jnp.min(code, axis=0, keepdims=True)
    chosen = jnp.min(least_ref[...], axis=1, keepdims=True).astype(jnp.int32)
    chosen = lax.rem(chosen, jnp.full_like(chosen, total))
    pick = (lax.broadcasted_iota(jnp.int32, (tiles, total), 1) == chosen).astype(jnp.float32)
    pick_out[...] = pick
    following = follow(pick, got_ref[:, :tiles, :].reshape(total, rows))
    own = own_ref[0, :tiles]
    for tile in range(tiles):
        nearby_out[tile] = gather_tile(own[tile:tile + 1], following[tile:tile + 1], codes_ref[tile], rows)


def first_sweep_kernel(*refs):
    *part_refs, nearby_ref, right_ref, diag_ref, vals_out, send_out = refs
    tiles = nearby_ref.shape[0]
    sums = []
    for tile in range(tiles):
        vals = part_refs[0][tile]
        for part in part_refs[1:]:
            vals = vals + part[tile]
        vals_out[tile] = vals
        sums.append(jnp.sum(vals * nearby_ref[tile], axis=0, keepdims=True))
    iterate = (right_ref[...] - jnp.concatenate(sums, axis=0)) / diag_ref[...]
    send_out[...] = jnp.broadcast_to(iterate[None], send_out.shape)


def sweep_kernel(got_ref, own_ref, pick_ref, codes_ref, vals_ref, right_ref, diag_ref, send_out):
    tiles, _, rows = codes_ref.shape
    following = follow(pick_ref[...], got_ref[...].reshape(-1, rows))
    own = own_ref[0]
    sums = []
    for tile in range(tiles):
        nearby = gather_tile(own[tile:tile + 1], following[tile:tile + 1], codes_ref[tile], rows)
        sums.append(jnp.sum(vals_ref[tile] * nearby, axis=0, keepdims=True))
    iterate = (right_ref[...] - jnp.concatenate(sums, axis=0)) / diag_ref[...]
    send_out[...] = jnp.broadcast_to(iterate[None], send_out.shape)


def call(kernel, shapes, *args, scratch=()):
    vmem = pl.BlockSpec(memory_space=pltpu.VMEM)
    shapes = [jax.ShapeDtypeStruct(shape, jnp.float32) for shape in shapes]
    return pl.pallas_call(
        kernel, out_shape=shapes, in_specs=[vmem] * len(args), out_specs=[vmem] * len(shapes), scratch_shapes=scratch
    )(*args)


def on_device(values, diagonal, rhs_parts, owner_map, columns, destination, order_keys):
    parts = lax.axis_size("src")
    me = lax.axis_index("src")
    peers = parts * lax.axis_size("blk")
    held, stored, rows = values.shape[1:]
    mine = held // parts
    vec = (mine, rows)
    mat = (mine, stored, rows)

    def cut(array, part):
        return lax.dynamic_slice_in_dim(array, part * mine, mine, 0)

    small = jnp.stack([diagonal[0].reshape((parts,) + vec), rhs_parts[0].reshape((parts,) + vec)], axis=1)
    got_small = lax.all_to_all(small, "src", 0, 0, tiled=True)
    pieces = [cut(values[0], me)]
    for step in range(1, parts):
        piece = cut(values[0], jnp.remainder(me + step, parts))
        pieces.append(lax.ppermute(piece, "src", [(i, (i + step) % parts) for i in range(parts)]))
    own_map = cut(owner_map, me)
    codes = cut(columns, me)
    own_owner = cut(destination, me).astype(jnp.float32)
    own_key = cut(order_keys[:, None], me).astype(jnp.float32)
    head = jnp.concatenate([own_owner.T, own_key.T], axis=0)
    head = jnp.pad(head, ((0, HEAD - 2), (0, rows - mine)), constant_values=-1.0)

    diag, right, send = call(start_kernel, [vec, vec, (peers, mine + HEAD, rows)], got_small, own_map, head)
    got = lax.all_to_all(send, BOTH, 0, 0, tiled=True)
    nearby, pick = call(
        nearby_kernel, [mat, (mine, mine * peers)], got, send, own_owner, own_key, codes,
        scratch=[pltpu.VMEM(vec, jnp.float32)],
    )
    vals, send = call(first_sweep_kernel, [mat, (peers,) + vec], *pieces, nearby, right, diag)
    for sweep in range(2, SWEEPS):
        last = sweep == SWEEPS - 1
        got = lax.all_to_all(send, BOTH, 0, 0, tiled=True)
        (send,) = call(sweep_kernel, [((1 if last else peers),) + vec], got, send, pick, codes, vals, right, diag)
    return lax.all_gather(send[0], "src", axis=0, tiled=True)


def solution(mesh):
    placed = (
        P("src", "blk", None, None),
        P("src", "blk", None),
        P("src", "blk", None),
        P("blk", None),
        P("blk", None, None),
        P("blk", None),
        P("blk"),
    )
    return jax.shard_map(
        on_device, mesh=mesh, in_specs=placed, out_specs=P("blk", None), check_vma=False
    )
```

time: 321 us -> 66.2 us (0.21)
  waiting for transfers between devices: 163 us -> 9.9 us
  other arithmetic: 82.2 us -> 3.6 us
  local copies, waits for them, and re-layouts: 27 us -> 7.01 us
  between operations: 14.7 us -> 0.08 us
  blocking collectives: 10.5 us -> 21.4 us
  Pallas kernels: 0 us -> 9.5 us
  starting transfers between devices: 22.7 us -> 14 us
    psum x3 -> x0, waiting for transfers between devices: 123 us -> none  [on_device(): summed = lax.psum(partial_sum, 'src')]
    reduce_sum x16 -> x0, other arithmetic: 73.1 us -> none  [the longest x8 45.3 us: build(): return jnp.sum(picked, axis=1)]
    all_to_all x5 -> x2, waiting for transfers between devices: 35.3 us -> 8.06 us  [the longest x1 6.77 us: on_device(): got = lax.all_to_all(send, BOTH, 0, 0, tiled=True)]
    gather x14 -> x0, local copies, waits for them, and re-layouts: 12.4 us -> none  [the longest x1 2.17 us: on_device(): send_cols = columns[source_tile]]
    dynamic_update_slice x8 -> x0, local copies, waits for them, and re-layouts: 12.3 us -> none  [tile_matrix(): dense = lax.map(build, (grouped_vals, grouped_lanes))]
    all_to_all x5 -> x2, starting transfers between devices: 22.4 us -> 10.2 us  [the longest x1 5.19 us: on_device(): got_small = lax.all_to_all(small, 'src', 0, 0, tiled=True)]
    pallas_call x0 -> x4, Pallas kernels: none -> 9.5 us  [call(): pl.pallas_call(kernel, out_shape=shapes, in_specs=[vmem] * len(args), out...]
    all_gather x0 -> x1, blocking collectives: none -> 7.54 us  [on_device(): return lax.all_gather(send[0], 'src', axis=0, tiled=True)]
  transfers between devices with their start and end apart: 9 -> 5, of which waited for: 9 -> 4; matrix products, arithmetic and copies ran while one was open for 4% -> 10% of each run, Pallas kernels for 0% -> 5%
where the time goes in v1:
time: 66.2 us; the launch traced here: 65.6 us
  blocking collectives  21.4 us (32%)
  starting transfers between devices  14 us (21%)
  waiting for transfers between devices  9.9 us (15%)
  Pallas kernels  9.5 us (14%)
  local copies, waits for them, and re-layouts  7.01 us (11%)
  other arithmetic  3.6 us (5%)
    all_to_all x1, blocking collectives, on_device(): got = lax.all_to_all(send, BOTH, 0, 0, tiled=True)  13.9 us
    pallas_call x4, Pallas kernels, call(): pl.pallas_call(kernel, out_shape=shapes, in_specs=[vmem] * len(args), out...  9.5 us
    all_gather x1, blocking collectives, on_device(): return lax.all_gather(send[0], 'src', axis=0, tiled=True)  7.54 us
    all_to_all x1, waiting for transfers between devices, on_device(): got = lax.all_to_all(send, BOTH, 0, 0, tiled=True)  6.77 us
    all_to_all x1, starting transfers between devices, on_device(): got_small = lax.all_to_all(small, 'src', 0, 0, tiled=True)  5.19 us
    all_to_all x1, starting transfers between devices, on_device(): got = lax.all_to_all(send, BOTH, 0, 0, tiled=True)  5.04 us
    ppermute x3, starting transfers between devices, on_device(): lax.ppermute(piece, 'src', [(i, (i + step) % parts) for i in range(parts)])  3.79 us
    dynamic_slice x4, local copies, waits for them, and re-layouts, cut(): return lax.dynamic_slice_in_dim(array, part * mine, mine, 0)  3.55 us
  transfers between devices with their start and end apart: 5, of which 4 were waited for; matrix products, arithmetic and copies ran while one was open for 10% of the time, Pallas kernels for 5%

profile of v1, /device:TPU:0, one launch (start us, length us, event | category | flops | bytes accessed | tf_op | source)
XLA Modules:
  0.0 65.6 jit_solution(12446395577875786502)
XLA Ops:
  0.0 0.0 copy-start
  0.0 0.0 copy-start.2
  0.0 1.5 %pad_maximum_fusion = f32[4,2,16,128]{3,2,1,0:T(8,128)} fusion(f32[4,1,16,128]{3,2,1,0:T(8,128)} %bitcast.17, f32[4,1,16,128]{3,2,1,0:T(8,128)} %bitcast.18), kind=kLoop, calls=%fused_computation.4 | loop fusion | flops 16384 | bytes 131072 | tf_op jit(solution)/shard_map/stack | solution.py:109
  1.6 5.2 %all-to-all-start = ((f32[4,2,16,128]{3,2,1,0:T(8,128)}), f32[4,2,16,128]{3,2,1,0:T(8,128)S(1)}, u32[]{:S(2)}, u32[]{:S(2)}) async-start(f32[4,2,16,128]{3,2,1,0:T(8,128)} %pad_maximum_fusion), calls=%async_computation | async-start | bytes 131072 | tf_op jit(solution)/shard_map/all_to_all | solution.py:110
  6.7 0.7 %constant_dynamic-slice_fusion.1 = s32[16,1]{0,1:T(1,128)S(1)} fusion(s32[64,1]{0,1:T(1,128)} %param.12, s32[]{:T(128)S(6)} %select_n.31), kind=kLoop, calls=%fused_computation.9 | loop fusion | bytes 132 | tf_op jit(solution)/shard_map/dynamic_slice | solution.py:107
  7.5 0.7 %convert_bitcast_fusion = (f32[16,1]{0,1:T(1,128)S(1)}, f32[1,16]{1,0:T(1,128)S(1)}) fusion(s32[64]{0:T(128)} %param.13, s32[]{:T(128)S(6)} %select_n.31), kind=kLoop, calls=%fused_computation.11 | loop fusion | flops 16 | bytes 196 | tf_op jit(solution)/shard_map/convert_element_type | solution.py:118
  8.2 0.1 copy.12
  8.3 0.1 convert_reduce_fusion
  8.4 1.3 %constant_dynamic-slice_fusion.2.owner_ref = s32[16,128]{1,0:T(8,128)} fusion(s32[64,128]{1,0:T(8,128)} %param.10, s32[]{:T(128)S(6)} %select_n.31), kind=kLoop, calls=%fused_computation.10 | loop fusion | bytes 16388 | tf_op jit(solution)/shard_map/dynamic_slice | solution.py:107
  9.7 0.6 select_maximum_fusion.head_ref
  10.3 1.3 %all-to-all-done.small_ref = f32[4,2,16,128]{3,2,1,0:T(8,128)S(1)} async-done(((f32[4,2,16,128]{3,2,1,0:T(8,128)}), f32[4,2,16,128]{3,2,1,0:T(8,128)S(1)}, u32[]{:S(2)}, u32[]{:S(2)}) %all-to-all-start) | async-done | bytes 65568 | tf_op jit(solution)/shard_map/all_to_all | solution.py:110
  11.6 0.0 copy-start.3
  11.6 0.6 copy-done.3
  12.2 1.6 %shard_map.73 = (f32[16,128]{1,0:T(8,128)}, f32[16,128]{1,0:T(8,128)}, f32[32,24,128]{2,1,0:T(8,128)}) custom-call(f32[4,2,16,128]{3,2,1,0:T(8,128)} %copy-done.3, s32[16,128]{1,0:T(8,128)} %constant_dynamic-slice_fusion.2.owner_ref, f32[8,128]{1,0:T(8,128)} %select_maximum_fusion.head_ref), custom_call_target="tpu_custom_call" | custom-call | tf_op jit(solution)/shard_map/pallas_call | solution.py:92
  13.9 5.0 %all-to-all-start.1 = ((f32[32,24,128]{2,1,0:T(8,128)}), f32[32,24,128]{2,1,0:T(8,128)S(1)}, u32[]{:S(2)}, u32[]{:S(2)}) async-start(f32[32,24,128]{2,1,0:T(8,128)} %get-tuple-element.12.own_ref), calls=%async_computation.1 | async-start | bytes 786432 | tf_op jit(solution)/shard_map/all_to_all | solution.py:123
  18.9 0.0 copy-done.2
  19.0 0.8 %dynamic-slice_bitcast_fusion = (f32[16,32,128]{2,1,0:T(8,128)S(1)}, f32[16,32,128]{2,1,0:T(8,128)S(1)}, f32[16,32,128]{2,1,0:T(8,128)}, f32[16,32,128]{2,1,0:T(8,128)S(1)}) fusion(f32[1,64,32,128]{3,2,1,0:T(8,128)S(1)} %copy-done.2, s32[]{:T(128)S(6)} %select_n.37, s32[]{:T(128)S(6)} %select_n.33, s32[]{:T(128)S(6)} %select_n.31, s32[]{:T(128)S(6)} %select_n.35), kind=kLoop, calls=%fused_computation | loop fusion | bytes 2097168 | tf_op jit(solution)/shard_map/dynamic_slice | solution.py:107
  19.8 2.7 %collective-permute-start.2 = (f32[16,32,128]{2,1,0:T(8,128)S(1)}, f32[16,32,128]{2,1,0:T(8,128)S(1)}, u32[]{:S(2)}, u32[]{:S(2)}) collective-permute-start(f32[16,32,128]{2,1,0:T(8,128)S(1)} %get-tuple-element.19), channel_id=1, source_target_pairs={{0,24},{8,0},{16,8},{24,16},{1,25},{9,1},{17,9},{25,17},{2,26},{10... | collective-permute-start | bytes 786440 | tf_op jit(solution)/shard_map/ppermute | solution.py:114
  22.4 0.0 collective-permute-start
  22.4 1.1 %collective-permute-start.1 = (f32[16,32,128]{2,1,0:T(8,128)S(1)}, f32[16,32,128]{2,1,0:T(8,128)S(1)}, u32[]{:S(2)}, u32[]{:S(2)}) collective-permute-start(f32[16,32,128]{2,1,0:T(8,128)S(1)} %get-tuple-element.22), channel_id=1, source_target_pairs={{0,16},{8,24},{16,0},{24,8},{1,17},{9,25},{17,1},{25,9},{2,18},{10... | collective-permute-start | bytes 786440 | tf_op jit(solution)/shard_map/ppermute | solution.py:114
  23.6 0.6 convert_element_type.8.owner_ref
  24.2 0.7 %copy.11.key_ref = f32[16,1]{1,0:T(8,128)} copy(f32[16,1]{0,1:T(1,128)S(1)} %get-tuple-element.23) | data formatting | bytes 128 | tf_op jit(solution)/shard_map/convert_element_type | solution.py:118
  24.8 0.0 copy-done
  24.8 0.7 %constant_dynamic-slice_fusion.codes_ref = s32[16,32,128]{2,1,0:T(8,128)} fusion(s32[64,32,128]{2,1,0:T(8,128)S(1)} %copy-done, s32[]{:T(128)S(6)} %select_n.31), kind=kLoop, calls=%fused_computation.8 | loop fusion | bytes 524292 | tf_op jit(solution)/shard_map/dynamic_slice | solution.py:107
  25.6 6.8 %all-to-all-done.1.got_ref = f32[32,24,128]{2,1,0:T(8,128)S(1)} async-done(((f32[32,24,128]{2,1,0:T(8,128)}), f32[32,24,128]{2,1,0:T(8,128)S(1)}, u32[]{:S(2)}, u32[]{:S(2)}) %all-to-all-start.1) | async-done | bytes 393248 | tf_op jit(solution)/shard_map/all_to_all | solution.py:123
  32.3 0.0 copy-start.1
  32.3 0.7 %copy-done.1 = f32[32,24,128]{2,1,0:T(8,128)} copy-done((f32[32,24,128]{2,1,0:T(8,128)}, f32[32,24,128]{2,1,0:T(8,128)S(1)}, u32[]{:S(2)}) %copy-start.1) | copy-done | bytes 393240
  33.1 3.4 %shard_map.74 = (f32[16,32,128]{2,1,0:T(8,128)}, f32[16,512]{1,0:T(8,128)}) custom-call(f32[32,24,128]{2,1,0:T(8,128)} %copy-done.1, f32[32,24,128]{2,1,0:T(8,128)} %get-tuple-element.12.own_ref, f32[16,1]{1,0:T(8,128)} %convert_element_type.8.owner_ref, f32[16,1]{1,0:T(8,128)} %copy.11.key_ref, s32[16,32,128]{2,1,0:T(8,128)} %constant_dynamic-slice_fusion.codes_ref), custom_call_target="tpu_custom_call" | custom-call | tf_op jit(solution)/shard_map/pallas_call | solution.py:92
  36.5 0.0 collective-permute-done.2.refs_3_
  36.5 0.0 copy-start.4
  36.5 1.6 %collective-permute-done.refs_1_ = f32[16,32,128]{2,1,0:T(8,128)S(1)} collective-permute-done((f32[16,32,128]{2,1,0:T(8,128)S(1)}, f32[16,32,128]{2,1,0:T(8,128)S(1)}, u32[]{:S(2)}, u32[]{:S(2)}) %collective-permute-start) | collective-permute-done | bytes 262176 | tf_op jit(solution)/shard_map/ppermute | solution.py:114
  38.1 0.0 copy-start.5
  38.1 0.2 collective-permute-done.1.refs_2_
  38.3 0.0 copy-start.6
  38.3 0.0 copy-done.4
  38.3 0.5 copy-done.5
  38.8 0.2 copy-done.6
  39.0 2.1 %shard_map.75 = (f32[16,32,128]{2,1,0:T(8,128)}, f32[32,16,128]{2,1,0:T(8,128)}) custom-call(f32[16,32,128]{2,1,0:T(8,128)} %get-tuple-element.21.refs_0_, f32[16,32,128]{2,1,0:T(8,128)} %copy-done.5, f32[16,32,128]{2,1,0:T(8,128)} %copy-done.6, f32[16,32,128]{2,1,0:T(8,128)} %copy-done.4, f32[16,32,128]{2,1,0:T(8,128)} %get-tuple-element.13.refs_4_, ...), custom_call_target="tpu_custom_call" | custom-call | tf_op jit(solution)/shard_map/pallas_call | solution.py:92
  41.2 13.9 %all_to_all.15.got_ref = f32[32,16,128]{2,1,0:T(8,128)} all-to-all(f32[32,16,128]{2,1,0:T(8,128)} %get-tuple-element.16.own_ref), channel_id=1, replica_groups=mesh['src'=4,'blk'=8] {'src','blk'}, dimensions={0} | all-to-all | bytes 524288 | tf_op jit(solution)/shard_map/all_to_all | solution.py:131
  55.1 2.3 %shard_map.76 = f32[1,16,128]{2,1,0:T(8,128)} custom-call(f32[32,16,128]{2,1,0:T(8,128)} %all_to_all.15.got_ref, f32[32,16,128]{2,1,0:T(8,128)} %get-tuple-element.16.own_ref, f32[16,512]{1,0:T(8,128)} %get-tuple-element.17.pick_ref, s32[16,32,128]{2,1,0:T(8,128)} %constant_dynamic-slice_fusion.codes_ref, f32[16,32,128]{2,1,0:T(8,128)} %get-tuple-element.18.vals_ref, ...), custom_call_target="tpu_custom_call" | custom-call | tf_op jit(solution)/shard_map/pallas_call | solution.py:92
  57.4 7.5 %all-gather = f32[1,64,128]{2,1,0:T(8,128)S(1)} all-gather(f32[1,16,128]{2,1,0:T(8,128)} %shard_map.76), channel_id=2, replica_groups=mesh['src'=4,'blk'=8] {'src'}, dimensions={1}, use_global_device_ids=true | all-gather | bytes 40960 | tf_op jit(solution)/shard_map/all_gather | solution.py:133
  64.9 0.6 copy.14
Async XLA Ops:
  0.0 24.8 %copy-start = (s32[64,32,128]{2,1,0:T(8,128)S(1)}, s32[64,32,128]{2,1,0:T(8,128)}, u32[]{:S(2)}) copy-start(s32[64,32,128]{2,1,0:T(8,128)} %param.11) | copy-start | bytes 3145732
  0.0 18.9 %copy-start.2 = (f32[1,64,32,128]{3,2,1,0:T(8,128)S(1)}, f32[1,64,32,128]{3,2,1,0:T(8,128)}, u32[]{:S(2)}) copy-start(f32[1,64,32,128]{3,2,1,0:T(8,128)} %param.7) | copy-start | bytes 3145732
  1.6 10.0 %all-to-all-start = ((f32[4,2,16,128]{3,2,1,0:T(8,128)}), f32[4,2,16,128]{3,2,1,0:T(8,128)S(1)}, u32[]{:S(2)}, u32[]{:S(2)}) async-start(f32[4,2,16,128]{3,2,1,0:T(8,128)} %pad_maximum_fusion), calls=%async_computation | async-start | bytes 131072 | tf_op jit(solution)/shard_map/all_to_all | solution.py:110
  11.6 0.6 copy-start.3
  13.9 18.5 %all-to-all-start.1 = ((f32[32,24,128]{2,1,0:T(8,128)}), f32[32,24,128]{2,1,0:T(8,128)S(1)}, u32[]{:S(2)}, u32[]{:S(2)}) async-start(f32[32,24,128]{2,1,0:T(8,128)} %get-tuple-element.12.own_ref), calls=%async_computation.1 | async-start | bytes 786432 | tf_op jit(solution)/shard_map/all_to_all | solution.py:123
  19.8 16.7 %collective-permute-start.2 = (f32[16,32,128]{2,1,0:T(8,128)S(1)}, f32[16,32,128]{2,1,0:T(8,128)S(1)}, u32[]{:S(2)}, u32[]{:S(2)}) collective-permute-start(f32[16,32,128]{2,1,0:T(8,128)S(1)} %get-tuple-element.19), channel_id=1, source_target_pairs={{0,24},{8,0},{16,8},{24,16},{1,25},{9,1},{17,9},{25,17},{2,26},{10... | collective-permute-start | bytes 786440 | tf_op jit(solution)/shard_map/ppermute | solution.py:114
  22.4 15.7 %collective-permute-start = (f32[16,32,128]{2,1,0:T(8,128)S(1)}, f32[16,32,128]{2,1,0:T(8,128)S(1)}, u32[]{:S(2)}, u32[]{:S(2)}) collective-permute-start(f32[16,32,128]{2,1,0:T(8,128)S(1)} %get-tuple-element.20), channel_id=1, source_target_pairs={{0,8},{8,16},{16,24},{24,0},{1,9},{9,17},{17,25},{25,1},{2,10},{10... | collective-permute-start | bytes 786440 | tf_op jit(solution)/shard_map/ppermute | solution.py:114
  22.4 15.9 %collective-permute-start.1 = (f32[16,32,128]{2,1,0:T(8,128)S(1)}, f32[16,32,128]{2,1,0:T(8,128)S(1)}, u32[]{:S(2)}, u32[]{:S(2)}) collective-permute-start(f32[16,32,128]{2,1,0:T(8,128)S(1)} %get-tuple-element.22), channel_id=1, source_target_pairs={{0,16},{8,24},{16,0},{24,8},{1,17},{9,25},{17,1},{25,9},{2,18},{10... | collective-permute-start | bytes 786440 | tf_op jit(solution)/shard_map/ppermute | solution.py:114
  32.3 0.8 %copy-start.1 = (f32[32,24,128]{2,1,0:T(8,128)}, f32[32,24,128]{2,1,0:T(8,128)S(1)}, u32[]{:S(2)}) copy-start(f32[32,24,128]{2,1,0:T(8,128)S(1)} %all-to-all-done.1.got_ref) | copy-start | bytes 1179652
  36.5 1.9 %copy-start.4 = (f32[16,32,128]{2,1,0:T(8,128)}, f32[16,32,128]{2,1,0:T(8,128)S(1)}, u32[]{:S(2)}) copy-start(f32[16,32,128]{2,1,0:T(8,128)S(1)} %collective-permute-done.2.refs_3_) | copy-start | bytes 786436
  38.1 0.7 %copy-start.5 = (f32[16,32,128]{2,1,0:T(8,128)}, f32[16,32,128]{2,1,0:T(8,128)S(1)}, u32[]{:S(2)}) copy-start(f32[16,32,128]{2,1,0:T(8,128)S(1)} %collective-permute-done.refs_1_) | copy-start | bytes 786436
  38.3 0.7 %copy-start.6 = (f32[16,32,128]{2,1,0:T(8,128)}, f32[16,32,128]{2,1,0:T(8,128)S(1)}, u32[]{:S(2)}) copy-start(f32[16,32,128]{2,1,0:T(8,128)S(1)} %collective-permute-done.1.refs_2_) | copy-start | bytes 786436
